TPU v7x, 32 devices: a whole 2x2x4 slice. The times are simulated.
32 devices in a mesh: section: 4 (over z), gx: 2 (over x), gy: 2 (over y), gz: 2 (over core).
Axes of the slice: x: 2, y: 2, z: 4, core: 2. Of those that a mesh axis runs over, the one named last changes fastest.
Arguments:
- micro_inputs: bfloat16 [1, 256, 8192], P(None, 'gy', ('gx', 'gz')), may hold values from -40 to 40
- norm_gain: float32 [4, 8192], P('section', 'gx'), may hold values from 0.5 to 1.5
- q_weight: bfloat16 [4, 8192, 8192], P('section', ('gx', 'gy'), 'gz'), may hold values from -0.0625 to 0.0625
- kv_weight: bfloat16 [4, 2, 8192, 1024], P('section', None, ('gx', 'gy'), 'gz'), may hold values from -0.0625 to 0.0625
- q_bias: float32 [4, 8192], P('section', 'gz'), may hold values from -130 to 130
- kv_bias: float32 [4, 2, 1024], P('section', None, 'gz'), may hold values from -50 to 50
- out_weight: bfloat16 [4, 8192, 8192], P('section', 'gz', ('gx', 'gy')), may hold values from -0.0625 to 0.0625
Outputs:
- hidden_out: bfloat16 [4, 1, 256, 8192], P('section', None, 'gy', ('gx', 'gz'))
All inputs are finite; a program needn't handle non-finite values.
Results may differ from a plain program's by a relative error of at most 0.025.
Values may be sent and summed in bfloat16 or wider, within the bound.
No kernel may reach another device: no remote copies, remote signals or barrier semaphores. Data moves between devices by JAX's collectives and lax.ppermute only.
A program may use at most 128 MiB of HBM per device.

v0:
```python
import jax
import jax.numpy as jnp
from jax import lax
from jax.sharding import PartitionSpec as P

D = 8192
HD = 128
ROPE_BASE = 1000000.0
EPSILON = 1e-06
NEG_FILL = -1e30


def from_behind(value, axis, steps):
    count = lax.axis_size(axis)
    initial, last = (max(0, -steps), min(count, count - steps))
    return lax.ppermute(value, axis, [(source, source + steps) for source in range(initial, last)])


def rotary(values, positions):
    half_width = values.shape[-1] // 2
    frequency = ROPE_BASE ** (-jnp.arange(half_width, dtype=jnp.float32) * 2.0 / values.shape[-1])
    angles = positions.astype(jnp.float32)[:, None] * frequency[None, :]
    cosine = jnp.cos(angles)[:, None, :]
    sine_part = jnp.sin(angles)[:, None, :]
    lower_half = values[..., :half_width]
    upper_half = values[..., half_width:]
    return jnp.concatenate(
        [
            lower_half * cosine - upper_half * sine_part,
            upper_half * cosine + lower_half * sine_part,
        ],
        axis=-1,
    )


def body(micro_inputs, norm_gain, q_weight, kv_weight, q_bias, kv_bias, out_weight):
    section_count = lax.axis_size("section")
    size_gx = lax.axis_size("gx")
    micro_count = micro_inputs.shape[0]
    local_rows = micro_inputs.shape[1]
    index_gx = lax.axis_index("gx")
    index_gy = lax.axis_index("gy")
    index_section = lax.axis_index("section")
    query_weight = q_weight[0]
    pair_weight = jnp.concatenate([kv_weight[0, 0], kv_weight[0, 1]], axis=1)
    mixing_weight = out_weight[0]
    slab_rows = q_weight.shape[1]
    q_cols = query_weight.shape[1]
    kv_cols = pair_weight.shape[1] // 2
    gain_row = norm_gain[0]
    q_heads = q_cols // HD
    kv_heads = kv_cols // HD
    group_size = q_heads // kv_heads
    own_cols = q_cols // size_gx
    own_heads = own_cols // HD
    if own_heads > group_size:
        used_heads = own_heads // group_size
        local_group = group_size
    else:
        used_heads = 1
        local_group = own_heads
    used_start = index_gx * own_heads // group_size
    score_scale = HD ** (-0.5)
    row_pos = index_gy * local_rows + jnp.arange(local_rows)
    own_bias = lax.dynamic_slice_in_dim(q_bias[0], index_gx * own_cols, own_cols, 0)

    def mix_cols(piece):
        return jnp.dot(piece, mixing_weight, preferred_element_type=jnp.float32)

    def attention_layer(wide_block):
        widened = wide_block.astype(jnp.float32)
        squares = lax.psum(jnp.sum(widened * widened, axis=1), "gx")
        normed = (widened * lax.rsqrt(squares / D + EPSILON)[:, None] * gain_row[None, :]).astype(
            jnp.bfloat16
        )
        all_tokens = lax.all_gather(normed, "gy", axis=0, tiled=True)
        own_slab = lax.dynamic_slice_in_dim(all_tokens, index_gy * slab_rows, slab_rows, 1)
        query_part = jnp.dot(own_slab, query_weight, preferred_element_type=jnp.float32)
        pair_part = jnp.dot(own_slab, pair_weight, preferred_element_type=jnp.float32)
        query_rows, pair_local = (
            lax.psum_scatter(
                query_part.astype(jnp.bfloat16), "gy", scatter_dimension=0, tiled=True
            ).astype(jnp.float32),
            lax.psum_scatter(
                pair_part.astype(jnp.bfloat16), "gy", scatter_dimension=0, tiled=True
            ).astype(jnp.float32),
        )
        queries = (
            lax.psum_scatter(
                query_rows.astype(jnp.bfloat16), "gx", scatter_dimension=1, tiled=True
            ).astype(jnp.float32)
            + own_bias[None, :]
        )
        pair_terms = lax.psum(pair_local.astype(jnp.bfloat16), "gx").astype(jnp.float32)
        key_rows = pair_terms[:, :kv_cols] + kv_bias[0, 0][None, :]
        value_rows = (pair_terms[:, kv_cols:] + kv_bias[0, 1][None, :]).astype(jnp.bfloat16)
        queries = rotary(queries.reshape(local_rows, own_heads, HD), row_pos).astype(jnp.bfloat16)
        queries = queries.reshape(local_rows, used_heads, local_group, HD)
        key_rows = rotary(key_rows.reshape(local_rows, kv_heads, HD), row_pos).astype(jnp.bfloat16)
        key_used = lax.dynamic_slice_in_dim(key_rows, used_start, used_heads, 1).reshape(
            local_rows, used_heads * HD
        )
        value_used = lax.dynamic_slice_in_dim(
            value_rows.reshape(local_rows, kv_heads, HD), used_start, used_heads, 1
        ).reshape(local_rows, used_heads * HD)
        running_max = jnp.full((used_heads, local_group, local_rows), NEG_FILL, jnp.float32)
        key_piece = lax.all_gather(key_used, "gy", axis=0, tiled=True)
        value_piece = lax.all_gather(value_used, "gy", axis=0, tiled=True)
        key_count = key_piece.shape[0]
        key_pos = jnp.arange(key_count)
        scores = (
            jnp.einsum(
                "qhgd,khd->hgqk",
                queries,
                key_piece.reshape(key_count, used_heads, HD),
                preferred_element_type=jnp.float32,
            )
            * score_scale
        )
        allowed = key_pos[None, :] <= row_pos[:, None]
        scores = jnp.where(allowed, scores, NEG_FILL)
        new_max = jnp.maximum(running_max, jnp.max(scores, axis=-1))
        weights = jnp.where(allowed, jnp.exp(scores - new_max[..., None]), 0.0)
        running_sum = jnp.sum(weights, axis=-1)
        update = jnp.einsum(
            "hgqk,khd->qhgd",
            weights.astype(jnp.bfloat16),
            value_piece.reshape(key_count, used_heads, HD),
            preferred_element_type=jnp.float32,
        )
        weighted = update
        running_max, running_sum, weighted = (new_max, running_sum, weighted)
        attended = (
            (weighted / jnp.transpose(running_sum, (2, 0, 1))[..., None])
            .astype(jnp.bfloat16)
            .reshape(local_rows, own_cols)
        )
        every_token = lax.all_gather(attended, "gy", axis=0, tiled=True)
        column_sums = mix_cols(lax.all_gather(every_token, "gx", axis=1, tiled=True))
        return lax.all_to_all(
            column_sums.astype(jnp.bfloat16), "gy", split_axis=0, concat_axis=1, tiled=True
        ).astype(column_sums.dtype)

    def record(stored, tick_index, result):
        micro_index = tick_index - index_section
        is_valid = (micro_index >= 0) & (micro_index < micro_count)
        clipped = jnp.clip(micro_index, 0, micro_count - 1)
        previous = lax.dynamic_index_in_dim(stored, clipped, 0, keepdims=False)
        return lax.dynamic_update_index_in_dim(
            stored, jnp.where(is_valid, result, previous), clipped, 0
        )

    tick_count = micro_count + section_count - 1
    stored_start = jnp.zeros(micro_inputs.shape, jnp.bfloat16)

    def advance(tick_index, state):
        carried, stored = state
        fresh = lax.dynamic_index_in_dim(
            micro_inputs, jnp.clip(tick_index, 0, micro_count - 1), 0, keepdims=False
        )
        current = jnp.where(index_section == 0, fresh, carried)
        wide_block = lax.all_gather(current, "gz", axis=1, tiled=True)
        summed = lax.psum_scatter(
            attention_layer(wide_block).astype(jnp.bfloat16), "gz", scatter_dimension=1, tiled=True
        ).astype(jnp.float32)
        result = (current.astype(jnp.float32) + summed).astype(jnp.bfloat16)
        stored = record(stored, tick_index, result)
        return (from_behind(result, "section", 1), stored)

    carry_start = jnp.zeros(micro_inputs.shape[1:], jnp.bfloat16)
    final_state = lax.fori_loop(0, tick_count, advance, (carry_start, stored_start))
    return final_state[1][None]


def solution(mesh):
    return jax.shard_map(
        body,
        mesh=mesh,
        in_specs=(
            P(None, "gy", ("gx", "gz")),
            P("section", "gx"),
            P("section", ("gx", "gy"), "gz"),
            P("section", None, ("gx", "gy"), "gz"),
            P("section", "gz"),
            P("section", None, "gz"),
            P("section", "gz", ("gx", "gy")),
        ),
        out_specs=P("section", None, "gy", ("gx", "gz")),
        check_vma=False,
    )
```

profile of v0, /device:TPU:0, one launch (start us, length us, event | category | flops | bytes accessed | tf_op | source)
XLA Modules:
  0.0 1107.2 jit_solution(5537659410085549743)
XLA Ops:
  12.5 1087.3 %while.19 = (s32[]{:T(128)}, bf16[128,2048]{1,0:T(8,128)(2,1)S(1)}, bf16[1,128,2048]{2,1,0:T(8,128)(2,1)S(1)}, pred[]{:T(512)}, bf16[1,128,2048]{2,1,0:T(8,128)(...) while((s32[]{:T(128)}, bf16[128,2048]{1,0:T(8,128)(2,1)S(1)}, ...), condition=%wide.region_10.11_spmd.clone.clone, body=%wide.region_0.10_spmd.clone.clone.sunk | while | flops 9950043136 | bytes 130518144 | solution.py:171
  13.5 13.2 %all-gather.5.cloned.1.call-done = bf16[128,4096]{1,0:T(8,128)(2,1)} async-done(((bf16[128,2048]{1,0:T(8,128)(2,1)}), bf16[128,4096]{1,0:T(8,128)(2,1)}) %all-gather.5.cloned.1.call-update) | async-done | bytes 1048592 | tf_op jit(solution)/shard_map/while/body/eval_jaxpr/all_gather | solution.py:162
  35.8 34.4 %all-gather.7.cloned.1.call-done = bf16[256,4096]{1,0:T(8,128)(2,1)} async-done(((bf16[128,4096]{1,0:T(8,128)(2,1)}), bf16[256,4096]{1,0:T(8,128)(2,1)}) %all-gather.7.cloned.1.call-update) | async-done | bytes 2097168 | tf_op jit(solution)/shard_map/while/body/eval_jaxpr/all_gather | solution.py:76
  74.8 12.0 %convolution_convert_fusion.7 = bf16[256,4096]{1,0:T(8,128)(2,1)} fusion(bf16[2048,4096]{1,0:T(8,128)(2,1)} %get-tuple-element.638, bf16[256,4096]{1,0:T(8,128)(2,1)} %all-gather.7.cloned.1.call-done, s32[]{:T(128)} %get-tuple-element.634), kind=kOutput, calls=%fused_computation.2.clone.1 | convolution fusion | flops 4296015872 | bytes 19923456 | tf_op jit(solution)/shard_map/while/body/eval_jaxpr/dot_general | solution.py:78
  89.7 34.0 %reduce-scatter.7.cloned.1.call-done = bf16[128,4096]{1,0:T(8,128)(2,1)} async-done(((bf16[256,4096]{1,0:T(8,128)(2,1)}), bf16[128,4096]{1,0:T(8,128)(2,1)}) %reduce-scatter.7.cloned.1.call-update) | async-done | bytes 1048592 | tf_op jit(solution)/shard_map/while/body/eval_jaxpr/reduce_scatter | solution.py:81
  124.1 25.0 %all-reduce.2.cloned.1.call-done = bf16[128,1024]{1,0:T(8,128)(2,1)} async-done(((bf16[128,1024]{1,0:T(8,128)(2,1)}), bf16[128,1024]{1,0:T(8,128)(2,1)}) %all-reduce.2.cloned.1.call-update) | async-done | bytes 262160 | tf_op jit(solution)/shard_map/while/body/eval_jaxpr/psum | solution.py:94
  176.5 21.4 %all-gather.9.cloned.1.call-done = bf16[256,2048]{0,1:T(8,128)(2,1)} async-done(((bf16[128,2048]{0,1:T(8,128)(2,1)}), bf16[256,2048]{0,1:T(8,128)(2,1)}) %all-gather.9.cloned.1.call-update) | async-done | bytes 1048592 | tf_op jit(solution)/shard_map/while/body/eval_jaxpr/all_gather | solution.py:138
  197.9 34.6 %all-gather.11.cloned.1.call-done = bf16[256,4096]{0,1:T(8,128)(2,1)} async-done(((bf16[256,2048]{0,1:T(8,128)(2,1)}), bf16[256,4096]{0,1:T(8,128)(2,1)}) %all-gather.11.cloned.1.call-update) | async-done | bytes 2097168 | tf_op jit(solution)/shard_map/while/body/eval_jaxpr/all_gather | solution.py:139
  243.5 16.2 %all_to_all.48 = bf16[2,128,2048]{2,1,0:T(8,128)(2,1)S(1)} all-to-all(bf16[2,128,2048]{2,1,0:T(8,128)(2,1)S(1)} %bitcast.132), channel_id=1, replica_groups=mesh['section'=4,'gx'=2,'gy'=2,'gz'=2] {'gy'}, dimensions={0} | all-to-all | bytes 2097152 | tf_op jit(solution)/shard_map/while/body/eval_jaxpr/all_to_all | solution.py:140
  285.9 12.1 %all-gather.5.cloned.1.call-done = bf16[128,4096]{1,0:T(8,128)(2,1)} async-done(((bf16[128,2048]{1,0:T(8,128)(2,1)}), bf16[128,4096]{1,0:T(8,128)(2,1)}) %all-gather.5.cloned.1.call-update) | async-done | bytes 1048592 | tf_op jit(solution)/shard_map/while/body/eval_jaxpr/all_gather | solution.py:162
  307.0 34.4 %all-gather.7.cloned.1.call-done = bf16[256,4096]{1,0:T(8,128)(2,1)} async-done(((bf16[128,4096]{1,0:T(8,128)(2,1)}), bf16[256,4096]{1,0:T(8,128)(2,1)}) %all-gather.7.cloned.1.call-update) | async-done | bytes 2097168 | tf_op jit(solution)/shard_map/while/body/eval_jaxpr/all_gather | solution.py:76
  346.1 12.0 %convolution_convert_fusion.7 = bf16[256,4096]{1,0:T(8,128)(2,1)} fusion(bf16[2048,4096]{1,0:T(8,128)(2,1)} %get-tuple-element.638, bf16[256,4096]{1,0:T(8,128)(2,1)} %all-gather.7.cloned.1.call-done, s32[]{:T(128)} %get-tuple-element.634), kind=kOutput, calls=%fused_computation.2.clone.1 | convolution fusion | flops 4296015872 | bytes 19923456 | tf_op jit(solution)/shard_map/while/body/eval_jaxpr/dot_general | solution.py:78
  360.9 34.1 %reduce-scatter.7.cloned.1.call-done = bf16[128,4096]{1,0:T(8,128)(2,1)} async-done(((bf16[256,4096]{1,0:T(8,128)(2,1)}), bf16[128,4096]{1,0:T(8,128)(2,1)}) %reduce-scatter.7.cloned.1.call-update) | async-done | bytes 1048592 | tf_op jit(solution)/shard_map/while/body/eval_jaxpr/reduce_scatter | solution.py:81
  395.5 25.0 %all-reduce.2.cloned.1.call-done = bf16[128,1024]{1,0:T(8,128)(2,1)} async-done(((bf16[128,1024]{1,0:T(8,128)(2,1)}), bf16[128,1024]{1,0:T(8,128)(2,1)}) %all-reduce.2.cloned.1.call-update) | async-done | bytes 262160 | tf_op jit(solution)/shard_map/while/body/eval_jaxpr/psum | solution.py:94
  447.9 21.4 %all-gather.9.cloned.1.call-done = bf16[256,2048]{0,1:T(8,128)(2,1)} async-done(((bf16[128,2048]{0,1:T(8,128)(2,1)}), bf16[256,2048]{0,1:T(8,128)(2,1)}) %all-gather.9.cloned.1.call-update) | async-done | bytes 1048592 | tf_op jit(solution)/shard_map/while/body/eval_jaxpr/all_gather | solution.py:138
  469.4 34.4 %all-gather.11.cloned.1.call-done = bf16[256,4096]{0,1:T(8,128)(2,1)} async-done(((bf16[256,2048]{0,1:T(8,128)(2,1)}), bf16[256,4096]{0,1:T(8,128)(2,1)}) %all-gather.11.cloned.1.call-update) | async-done | bytes 2097168 | tf_op jit(solution)/shard_map/while/body/eval_jaxpr/all_gather | solution.py:139
  514.7 16.2 %all_to_all.48 = bf16[2,128,2048]{2,1,0:T(8,128)(2,1)S(1)} all-to-all(bf16[2,128,2048]{2,1,0:T(8,128)(2,1)S(1)} %bitcast.132), channel_id=1, replica_groups=mesh['section'=4,'gx'=2,'gy'=2,'gz'=2] {'gy'}, dimensions={0} | all-to-all | bytes 2097152 | tf_op jit(solution)/shard_map/while/body/eval_jaxpr/all_to_all | solution.py:140
  557.1 12.4 %all-gather.5.cloned.1.call-done = bf16[128,4096]{1,0:T(8,128)(2,1)} async-done(((bf16[128,2048]{1,0:T(8,128)(2,1)}), bf16[128,4096]{1,0:T(8,128)(2,1)}) %all-gather.5.cloned.1.call-update) | async-done | bytes 1048592 | tf_op jit(solution)/shard_map/while/body/eval_jaxpr/all_gather | solution.py:162
  578.6 34.4 %all-gather.7.cloned.1.call-done = bf16[256,4096]{1,0:T(8,128)(2,1)} async-done(((bf16[128,4096]{1,0:T(8,128)(2,1)}), bf16[256,4096]{1,0:T(8,128)(2,1)}) %all-gather.7.cloned.1.call-update) | async-done | bytes 2097168 | tf_op jit(solution)/shard_map/while/body/eval_jaxpr/all_gather | solution.py:76
  617.7 12.0 %convolution_convert_fusion.7 = bf16[256,4096]{1,0:T(8,128)(2,1)} fusion(bf16[2048,4096]{1,0:T(8,128)(2,1)} %get-tuple-element.638, bf16[256,4096]{1,0:T(8,128)(2,1)} %all-gather.7.cloned.1.call-done, s32[]{:T(128)} %get-tuple-element.634), kind=kOutput, calls=%fused_computation.2.clone.1 | convolution fusion | flops 4296015872 | bytes 19923456 | tf_op jit(solution)/shard_map/while/body/eval_jaxpr/dot_general | solution.py:78
  632.5 34.1 %reduce-scatter.7.cloned.1.call-done = bf16[128,4096]{1,0:T(8,128)(2,1)} async-done(((bf16[256,4096]{1,0:T(8,128)(2,1)}), bf16[128,4096]{1,0:T(8,128)(2,1)}) %reduce-scatter.7.cloned.1.call-update) | async-done | bytes 1048592 | tf_op jit(solution)/shard_map/while/body/eval_jaxpr/reduce_scatter | solution.py:81
  667.1 25.1 %all-reduce.2.cloned.1.call-done = bf16[128,1024]{1,0:T(8,128)(2,1)} async-done(((bf16[128,1024]{1,0:T(8,128)(2,1)}), bf16[128,1024]{1,0:T(8,128)(2,1)}) %all-reduce.2.cloned.1.call-update) | async-done | bytes 262160 | tf_op jit(solution)/shard_map/while/body/eval_jaxpr/psum | solution.py:94
  719.7 21.4 %all-gather.9.cloned.1.call-done = bf16[256,2048]{0,1:T(8,128)(2,1)} async-done(((bf16[128,2048]{0,1:T(8,128)(2,1)}), bf16[256,2048]{0,1:T(8,128)(2,1)}) %all-gather.9.cloned.1.call-update) | async-done | bytes 1048592 | tf_op jit(solution)/shard_map/while/body/eval_jaxpr/all_gather | solution.py:138
  741.1 34.4 %all-gather.11.cloned.1.call-done = bf16[256,4096]{0,1:T(8,128)(2,1)} async-done(((bf16[256,2048]{0,1:T(8,128)(2,1)}), bf16[256,4096]{0,1:T(8,128)(2,1)}) %all-gather.11.cloned.1.call-update) | async-done | bytes 2097168 | tf_op jit(solution)/shard_map/while/body/eval_jaxpr/all_gather | solution.py:139
  786.4 16.2 %all_to_all.48 = bf16[2,128,2048]{2,1,0:T(8,128)(2,1)S(1)} all-to-all(bf16[2,128,2048]{2,1,0:T(8,128)(2,1)S(1)} %bitcast.132), channel_id=1, replica_groups=mesh['section'=4,'gx'=2,'gy'=2,'gz'=2] {'gy'}, dimensions={0} | all-to-all | bytes 2097152 | tf_op jit(solution)/shard_map/while/body/eval_jaxpr/all_to_all | solution.py:140
  828.9 12.4 %all-gather.5.cloned.1.call-done = bf16[128,4096]{1,0:T(8,128)(2,1)} async-done(((bf16[128,2048]{1,0:T(8,128)(2,1)}), bf16[128,4096]{1,0:T(8,128)(2,1)}) %all-gather.5.cloned.1.call-update) | async-done | bytes 1048592 | tf_op jit(solution)/shard_map/while/body/eval_jaxpr/all_gather | solution.py:162
  850.4 34.4 %all-gather.7.cloned.1.call-done = bf16[256,4096]{1,0:T(8,128)(2,1)} async-done(((bf16[128,4096]{1,0:T(8,128)(2,1)}), bf16[256,4096]{1,0:T(8,128)(2,1)}) %all-gather.7.cloned.1.call-update) | async-done | bytes 2097168 | tf_op jit(solution)/shard_map/while/body/eval_jaxpr/all_gather | solution.py:76
  904.2 34.1 %reduce-scatter.7.cloned.1.call-done = bf16[128,4096]{1,0:T(8,128)(2,1)} async-done(((bf16[256,4096]{1,0:T(8,128)(2,1)}), bf16[128,4096]{1,0:T(8,128)(2,1)}) %reduce-scatter.7.cloned.1.call-update) | async-done | bytes 1048592 | tf_op jit(solution)/shard_map/while/body/eval_jaxpr/reduce_scatter | solution.py:81
  938.8 25.1 %all-reduce.2.cloned.1.call-done = bf16[128,1024]{1,0:T(8,128)(2,1)} async-done(((bf16[128,1024]{1,0:T(8,128)(2,1)}), bf16[128,1024]{1,0:T(8,128)(2,1)}) %all-reduce.2.cloned.1.call-update) | async-done | bytes 262160 | tf_op jit(solution)/shard_map/while/body/eval_jaxpr/psum | solution.py:94
  991.4 21.4 %all-gather.9.cloned.1.call-done = bf16[256,2048]{0,1:T(8,128)(2,1)} async-done(((bf16[128,2048]{0,1:T(8,128)(2,1)}), bf16[256,2048]{0,1:T(8,128)(2,1)}) %all-gather.9.cloned.1.call-update) | async-done | bytes 1048592 | tf_op jit(solution)/shard_map/while/body/eval_jaxpr/all_gather | solution.py:138
  1012.8 34.6 %all-gather.11.cloned.1.call-done = bf16[256,4096]{0,1:T(8,128)(2,1)} async-done(((bf16[256,2048]{0,1:T(8,128)(2,1)}), bf16[256,4096]{0,1:T(8,128)(2,1)}) %all-gather.11.cloned.1.call-update) | async-done | bytes 2097168 | tf_op jit(solution)/shard_map/while/body/eval_jaxpr/all_gather | solution.py:139
  1058.3 16.2 %all_to_all.48 = bf16[2,128,2048]{2,1,0:T(8,128)(2,1)S(1)} all-to-all(bf16[2,128,2048]{2,1,0:T(8,128)(2,1)S(1)} %bitcast.132), channel_id=1, replica_groups=mesh['section'=4,'gx'=2,'gy'=2,'gz'=2] {'gy'}, dimensions={0} | all-to-all | bytes 2097152 | tf_op jit(solution)/shard_map/while/body/eval_jaxpr/all_to_all | solution.py:140
  (254 shorter events, 344.5 us)
Async XLA Ops:
  13.5 56.7 %all-gather.7.cloned.1.call-start = ((), (), s32[]{:S(2)}) async-start(), calls=%async_computation.6 | async-start | bytes 3145728 | tf_op jit(solution)/shard_map/while/body/eval_jaxpr/all_gather | solution.py:76
  35.7 53.9 %reduce-scatter.5.cloned.1.call-start = ((), (), s32[]{:S(2)}) async-start(), calls=%async_computation.7 | async-start | bytes 786432 | tf_op jit(solution)/shard_map/while/body/eval_jaxpr/reduce_scatter | solution.py:84
  74.8 48.8 %reduce-scatter.7.cloned.1.call-start = ((), (), s32[]{:S(2)}) async-start(), calls=%async_computation.9 | async-start | bytes 3145728 | tf_op jit(solution)/shard_map/while/body/eval_jaxpr/reduce_scatter | solution.py:81
  86.8 62.2 %all-reduce.2.cloned.1.call-start = ((), (), s32[]{:S(2)}) async-start(), calls=%async_computation.8 | async-start | bytes 524288 | tf_op jit(solution)/shard_map/while/body/eval_jaxpr/psum | solution.py:94
  89.6 82.0 %reduce-scatter.9.cloned.1.call-start = ((), (), s32[]{:S(2)}) async-start(), calls=%async_computation.10 | async-start | bytes 1572864 | tf_op jit(solution)/shard_map/while/body/eval_jaxpr/reduce_scatter | solution.py:89
  123.7 74.2 %all-gather.9.cloned.1.call-start = ((), (), s32[]{:S(2)}) async-start(), calls=%async_computation.11 | async-start | bytes 1572864 | tf_op jit(solution)/shard_map/while/body/eval_jaxpr/all_gather | solution.py:138
  176.5 56.1 %all-gather.11.cloned.1.call-start = ((), (), s32[]{:S(2)}) async-start(), calls=%async_computation.12 | async-start | bytes 3145728 | tf_op jit(solution)/shard_map/while/body/eval_jaxpr/all_gather | solution.py:139
  197.9 70.4 %reduce-scatter.11.cloned.1.call-start = ((), (), s32[]{:S(2)}) async-start(), calls=%async_computation.13 | async-start | bytes 1572864 | tf_op jit(solution)/shard_map/while/body/eval_jaxpr/reduce_scatter | solution.py:163
  285.8 55.6 %all-gather.7.cloned.1.call-start = ((), (), s32[]{:S(2)}) async-start(), calls=%async_computation.6 | async-start | bytes 3145728 | tf_op jit(solution)/shard_map/while/body/eval_jaxpr/all_gather | solution.py:76
  307.0 53.9 %reduce-scatter.5.cloned.1.call-start = ((), (), s32[]{:S(2)}) async-start(), calls=%async_computation.7 | async-start | bytes 786432 | tf_op jit(solution)/shard_map/while/body/eval_jaxpr/reduce_scatter | solution.py:84
  346.1 49.0 %reduce-scatter.7.cloned.1.call-start = ((), (), s32[]{:S(2)}) async-start(), calls=%async_computation.9 | async-start | bytes 3145728 | tf_op jit(solution)/shard_map/while/body/eval_jaxpr/reduce_scatter | solution.py:81
  358.1 62.4 %all-reduce.2.cloned.1.call-start = ((), (), s32[]{:S(2)}) async-start(), calls=%async_computation.8 | async-start | bytes 524288 | tf_op jit(solution)/shard_map/while/body/eval_jaxpr/psum | solution.py:94
  360.9 82.1 %reduce-scatter.9.cloned.1.call-start = ((), (), s32[]{:S(2)}) async-start(), calls=%async_computation.10 | async-start | bytes 1572864 | tf_op jit(solution)/shard_map/while/body/eval_jaxpr/reduce_scatter | solution.py:89
  395.1 74.2 %all-gather.9.cloned.1.call-start = ((), (), s32[]{:S(2)}) async-start(), calls=%async_computation.11 | async-start | bytes 1572864 | tf_op jit(solution)/shard_map/while/body/eval_jaxpr/all_gather | solution.py:138
  447.9 55.9 %all-gather.11.cloned.1.call-start = ((), (), s32[]{:S(2)}) async-start(), calls=%async_computation.12 | async-start | bytes 3145728 | tf_op jit(solution)/shard_map/while/body/eval_jaxpr/all_gather | solution.py:139
  469.3 70.3 %reduce-scatter.11.cloned.1.call-start = ((), (), s32[]{:S(2)}) async-start(), calls=%async_computation.13 | async-start | bytes 1572864 | tf_op jit(solution)/shard_map/while/body/eval_jaxpr/reduce_scatter | solution.py:163
  557.1 55.9 %all-gather.7.cloned.1.call-start = ((), (), s32[]{:S(2)}) async-start(), calls=%async_computation.6 | async-start | bytes 3145728 | tf_op jit(solution)/shard_map/while/body/eval_jaxpr/all_gather | solution.py:76
  578.6 53.9 %reduce-scatter.5.cloned.1.call-start = ((), (), s32[]{:S(2)}) async-start(), calls=%async_computation.7 | async-start | bytes 786432 | tf_op jit(solution)/shard_map/while/body/eval_jaxpr/reduce_scatter | solution.py:84
  617.6 49.0 %reduce-scatter.7.cloned.1.call-start = ((), (), s32[]{:S(2)}) async-start(), calls=%async_computation.9 | async-start | bytes 3145728 | tf_op jit(solution)/shard_map/while/body/eval_jaxpr/reduce_scatter | solution.py:81
  629.7 62.5 %all-reduce.2.cloned.1.call-start = ((), (), s32[]{:S(2)}) async-start(), calls=%async_computation.8 | async-start | bytes 524288 | tf_op jit(solution)/shard_map/while/body/eval_jaxpr/psum | solution.py:94
  632.5 82.3 %reduce-scatter.9.cloned.1.call-start = ((), (), s32[]{:S(2)}) async-start(), calls=%async_computation.10 | async-start | bytes 1572864 | tf_op jit(solution)/shard_map/while/body/eval_jaxpr/reduce_scatter | solution.py:89
  666.6 74.4 %all-gather.9.cloned.1.call-start = ((), (), s32[]{:S(2)}) async-start(), calls=%async_computation.11 | async-start | bytes 1572864 | tf_op jit(solution)/shard_map/while/body/eval_jaxpr/all_gather | solution.py:138
  719.6 55.9 %all-gather.11.cloned.1.call-start = ((), (), s32[]{:S(2)}) async-start(), calls=%async_computation.12 | async-start | bytes 3145728 | tf_op jit(solution)/shard_map/while/body/eval_jaxpr/all_gather | solution.py:139
  741.0 70.3 %reduce-scatter.11.cloned.1.call-start = ((), (), s32[]{:S(2)}) async-start(), calls=%async_computation.13 | async-start | bytes 1572864 | tf_op jit(solution)/shard_map/while/body/eval_jaxpr/reduce_scatter | solution.py:163
  828.8 55.9 %all-gather.7.cloned.1.call-start = ((), (), s32[]{:S(2)}) async-start(), calls=%async_computation.6 | async-start | bytes 3145728 | tf_op jit(solution)/shard_map/while/body/eval_jaxpr/all_gather | solution.py:76
  850.3 53.9 %reduce-scatter.5.cloned.1.call-start = ((), (), s32[]{:S(2)}) async-start(), calls=%async_computation.7 | async-start | bytes 786432 | tf_op jit(solution)/shard_map/while/body/eval_jaxpr/reduce_scatter | solution.py:84
  889.4 49.0 %reduce-scatter.7.cloned.1.call-start = ((), (), s32[]{:S(2)}) async-start(), calls=%async_computation.9 | async-start | bytes 3145728 | tf_op jit(solution)/shard_map/while/body/eval_jaxpr/reduce_scatter | solution.py:81
  901.4 62.5 %all-reduce.2.cloned.1.call-start = ((), (), s32[]{:S(2)}) async-start(), calls=%async_computation.8 | async-start | bytes 524288 | tf_op jit(solution)/shard_map/while/body/eval_jaxpr/psum | solution.py:94
  904.2 82.3 %reduce-scatter.9.cloned.1.call-start = ((), (), s32[]{:S(2)}) async-start(), calls=%async_computation.10 | async-start | bytes 1572864 | tf_op jit(solution)/shard_map/while/body/eval_jaxpr/reduce_scatter | solution.py:89
  938.4 74.4 %all-gather.9.cloned.1.call-start = ((), (), s32[]{:S(2)}) async-start(), calls=%async_computation.11 | async-start | bytes 1572864 | tf_op jit(solution)/shard_map/while/body/eval_jaxpr/all_gather | solution.py:138
  991.4 56.1 %all-gather.11.cloned.1.call-start = ((), (), s32[]{:S(2)}) async-start(), calls=%async_computation.12 | async-start | bytes 3145728 | tf_op jit(solution)/shard_map/while/body/eval_jaxpr/all_gather | solution.py:139
  1012.8 70.4 %reduce-scatter.11.cloned.1.call-start = ((), (), s32[]{:S(2)}) async-start(), calls=%async_computation.13 | async-start | bytes 1572864 | tf_op jit(solution)/shard_map/while/body/eval_jaxpr/reduce_scatter | solution.py:163
  (18 other events, 160.3 us)
Sparse Core Ops, SparseCore 0:
  14.9 11.7 all-gather.4
  35.8 34.2 all-gather.6
  74.9 14.6 reduce-scatter.4
  91.7 31.8 reduce-scatter.6
  125.7 23.2 all-reduce.1
  151.2 20.3 reduce-scatter.8
  176.6 21.2 all-gather.8
  199.4 33.0 all-gather.10
  287.0 10.9 all-gather.4
  307.1 34.2 all-gather.6
  346.2 14.6 reduce-scatter.4
  363.1 31.8 reduce-scatter.6
  397.2 23.2 all-reduce.1
  422.6 20.3 reduce-scatter.8
  448.0 21.2 all-gather.8
  470.7 33.0 all-gather.10
  558.6 10.9 all-gather.4
  578.7 34.2 all-gather.6
  617.7 14.6 reduce-scatter.4
  634.7 31.8 reduce-scatter.6
  668.9 23.2 all-reduce.1
  694.3 20.3 reduce-scatter.8
  719.7 21.2 all-gather.8
  742.4 33.0 all-gather.10
  830.3 10.9 all-gather.4
  850.4 34.2 all-gather.6
  889.5 14.6 reduce-scatter.4
  906.4 31.8 reduce-scatter.6
  940.6 23.2 all-reduce.1
  966.1 20.3 reduce-scatter.8
  991.5 21.2 all-gather.8
  1014.3 33.0 all-gather.10
  (4 shorter events, 29.6 us)
where the time goes:
time: 1110 us
  waiting for transfers between devices  778 us (70%)
  blocking collectives  124 us (11%)
  matrix products  118 us (11%)
  other arithmetic  44.3 us (4%)
  starting transfers between devices  16.1 us (1%)
  between operations  13.1 us (1%)
  local copies, waits for them, and re-layouts  11.5 us (1%)
    all_gather x4, waiting for transfers between devices, attention_layer(): lax.all_gather(every_token, 'gx', axis=1, tiled=True)  138 us
    all_gather x4, waiting for transfers between devices, attention_layer(): all_tokens = lax.all_gather(normed, 'gy', axis=0, tiled=True)  138 us
    reduce_scatter x4, waiting for transfers between devices, attention_layer(): lax.psum_scatter(query_part.astype(jnp.bfloat16), 'gy', scatter_dimension...  136 us
    psum x4, waiting for transfers between devices, attention_layer(): lax.psum(pair_local.astype(jnp.bfloat16), 'gx').astype(jnp.float32)  100 us
    all_gather x4, waiting for transfers between devices, attention_layer(): every_token = lax.all_gather(attended, 'gy', axis=0, tiled=True)  85.4 us
    all_to_all x4, blocking collectives, attention_layer(): lax.all_to_all(column_sums.astype(jnp.bfloat16), 'gy', split_axis=0, conc...  64.7 us
    all_gather x4, waiting for transfers between devices, advance(): wide_block = lax.all_gather(current, 'gz', axis=1, tiled=True)  50.1 us
    dot_general x4, matrix products, attention_layer(): jnp.dot(own_slab, query_weight, preferred_element_type=jnp.float32)  47.9 us
  transfers between devices with their start and end apart: 40, of which 40 were waited for; matrix products, arithmetic and copies ran while one was open for 5% of the time, Pallas kernels for 0%

commit v1 on v0

--- a/solution.py
+++ b/solution.py
@@ -73,7 +73,10 @@
         normed = (widened * lax.rsqrt(squares / D + EPSILON)[:, None] * gain_row[None, :]).astype(
             jnp.bfloat16
         )
-        all_tokens = lax.all_gather(normed, "gy", axis=0, tiled=True)
+        size = lax.axis_size("gy")
+        blocks = jnp.stack([normed for _ in range(size)])
+        blocks = lax.all_to_all(blocks, "gy", split_axis=0, concat_axis=0)
+        all_tokens = jnp.concatenate(blocks, axis=0)
         own_slab = lax.dynamic_slice_in_dim(all_tokens, index_gy * slab_rows, slab_rows, 1)
         query_part = jnp.dot(own_slab, query_weight, preferred_element_type=jnp.float32)
         pair_part = jnp.dot(own_slab, pair_weight, preferred_element_type=jnp.float32)

time: 1110 us -> 1070 us (0.964)
  waiting for transfers between devices: 778 us -> 640 us
  blocking collectives: 124 us -> 233 us
    all_gather x4 -> x0, waiting for transfers between devices: 138 us -> none  [attention_layer(): all_tokens = lax.all_gather(normed, 'gy', axis=0, tiled=True)]
    all_to_all x0 -> x4, blocking collectives: none -> 109 us  [attention_layer(): blocks = lax.all_to_all(blocks, 'gy', split_axis=0, concat_axis=0)]
  transfers between devices with their start and end apart: 40 -> 36, of which waited for: 40 -> 36; matrix products, arithmetic and copies ran while one was open for 5% -> 5% of each run, Pallas kernels for 0% -> 0%
where the time goes in v1:
time: 1070 us
  waiting for transfers between devices  640 us (60%)
  blocking collectives  233 us (22%)
  matrix products  107 us (10%)
  other arithmetic  45.2 us (4%)
  starting transfers between devices  16 us (1%)
  between operations  13.1 us (1%)
  local copies, waits for them, and re-layouts  11.5 us (1%)
    all_gather x4, waiting for transfers between devices, attention_layer(): lax.all_gather(every_token, 'gx', axis=1, tiled=True)  138 us
    reduce_scatter x4, waiting for transfers between devices, attention_layer(): lax.psum_scatter(query_part.astype(jnp.bfloat16), 'gy', scatter_dimension...  137 us
    all_to_all x4, blocking collectives, attention_layer(): blocks = lax.all_to_all(blocks, 'gy', split_axis=0, concat_axis=0)  109 us
    psum x4, waiting for transfers between devices, attention_layer(): lax.psum(pair_local.astype(jnp.bfloat16), 'gx').astype(jnp.float32)  100 us
    all_gather x4, waiting for transfers between devices, attention_layer(): every_token = lax.all_gather(attended, 'gy', axis=0, tiled=True)  85.4 us
    all_to_all x4, blocking collectives, attention_layer(): lax.all_to_all(column_sums.astype(jnp.bfloat16), 'gy', split_axis=0, conc...  64.7 us
    ppermute x4, waiting for transfers between devices, from_behind(): lax.ppermute(value, axis, [(source, source + steps) for source in range(i...  46.3 us
    dot_general x4, matrix products, attention_layer(): jnp.dot(own_slab, query_weight, preferred_element_type=jnp.float32)  46 us
  transfers between devices with their start and end apart: 36, of which 36 were waited for; matrix products, arithmetic and copies ran while one was open for 5% of the time, Pallas kernels for 0%

profile of v1, /device:TPU:0, one launch (start us, length us, event | category | flops | bytes accessed | tf_op | source)
XLA Modules:
  0.0 1066.7 jit_solution(6620930910813246326)
XLA Ops:
  12.5 1046.8 %while.19 = (s32[]{:T(128)}, bf16[128,2048]{1,0:T(8,128)(2,1)S(1)}, bf16[1,128,2048]{2,1,0:T(8,128)(2,1)S(1)}, pred[]{:T(512)}, bf16[1,128,2048]{2,1,0:T(8,128)(...) while((s32[]{:T(128)}, bf16[128,2048]{1,0:T(8,128)(2,1)S(1)}, ...), condition=%wide.region_10.11_spmd.clone.clone, body=%wide.region_0.10_spmd.clone.clone.sunk | while | flops 9951091712 | bytes 145197168 | solution.py:174
  14.5 12.1 %all-gather.4.cloned.1.call-done = bf16[128,4096]{1,0:T(8,128)(2,1)} async-done(((bf16[128,2048]{1,0:T(8,128)(2,1)}), bf16[128,4096]{1,0:T(8,128)(2,1)}) %all-gather.4.cloned.1.call-update) | async-done | bytes 1048592 | tf_op jit(solution)/shard_map/while/body/eval_jaxpr/all_gather | solution.py:165
  34.9 27.2 %all_to_all.63 = bf16[2,128,4096]{2,1,0:T(8,128)(2,1)S(1)} all-to-all(bf16[2,128,4096]{2,1,0:T(8,128)(2,1)S(1)} %pad_maximum_fusion.3), channel_id=1, replica_groups=mesh['section'=4,'gx'=2,'gy'=2,'gz'=2] {'gy'}, dimensions={0} | all-to-all | bytes 4194304 | tf_op jit(solution)/shard_map/while/body/eval_jaxpr/all_to_all | solution.py:78
  64.3 11.5 %convolution_convert_fusion.7 = bf16[256,4096]{1,0:T(8,128)(2,1)} fusion(bf16[2048,4096]{1,0:T(8,128)(2,1)} %get-tuple-element.638, bf16[256,4096]{1,0:T(8,128)(2,1)S(1)} %bitcast.145, s32[]{:T(128)} %get-tuple-element.634), kind=kOutput, calls=%fused_computation.2.clone.1 | convolution fusion | flops 4296015872 | bytes 19922948 | tf_op jit(solution)/shard_map/while/body/eval_jaxpr/dot_general | solution.py:81
  79.3 34.2 %reduce-scatter.7.cloned.1.call-done = bf16[128,4096]{1,0:T(8,128)(2,1)} async-done(((bf16[256,4096]{1,0:T(8,128)(2,1)}), bf16[128,4096]{1,0:T(8,128)(2,1)}) %reduce-scatter.7.cloned.1.call-update) | async-done | bytes 1048592 | tf_op jit(solution)/shard_map/while/body/eval_jaxpr/reduce_scatter | solution.py:84
  114.0 25.0 %all-reduce.2.cloned.1.call-done = bf16[128,1024]{1,0:T(8,128)(2,1)} async-done(((bf16[128,1024]{1,0:T(8,128)(2,1)}), bf16[128,1024]{1,0:T(8,128)(2,1)}) %all-reduce.2.cloned.1.call-update) | async-done | bytes 262160 | tf_op jit(solution)/shard_map/while/body/eval_jaxpr/psum | solution.py:97
  166.4 21.4 %all-gather.6.cloned.1.call-done = bf16[256,2048]{0,1:T(8,128)(2,1)} async-done(((bf16[128,2048]{0,1:T(8,128)(2,1)}), bf16[256,2048]{0,1:T(8,128)(2,1)}) %all-gather.6.cloned.1.call-update) | async-done | bytes 1048592 | tf_op jit(solution)/shard_map/while/body/eval_jaxpr/all_gather | solution.py:141
  187.8 34.6 %all-gather.8.cloned.1.call-done = bf16[256,4096]{0,1:T(8,128)(2,1)} async-done(((bf16[256,2048]{0,1:T(8,128)(2,1)}), bf16[256,4096]{0,1:T(8,128)(2,1)}) %all-gather.8.cloned.1.call-update) | async-done | bytes 2097168 | tf_op jit(solution)/shard_map/while/body/eval_jaxpr/all_gather | solution.py:142
  233.3 16.2 %all_to_all.64 = bf16[2,128,2048]{2,1,0:T(8,128)(2,1)S(1)} all-to-all(bf16[2,128,2048]{2,1,0:T(8,128)(2,1)S(1)} %bitcast.139), channel_id=1, replica_groups=mesh['section'=4,'gx'=2,'gy'=2,'gz'=2] {'gy'}, dimensions={0} | all-to-all | bytes 2097152 | tf_op jit(solution)/shard_map/while/body/eval_jaxpr/all_to_all | solution.py:143
  263.3 11.6 %collective-permute-done = bf16[128,2048]{1,0:T(8,128)(2,1)S(1)} collective-permute-done((bf16[128,2048]{1,0:T(8,128)(2,1)S(1)}, bf16[128,2048]{1,0:T(8,128)(2,1)S(1)}, u32[]{:S(2)}, u32[]{:S(2)}) %collective-permute-start) | collective-permute-done | bytes 524320 | tf_op jit(solution)/shard_map/while/body/eval_jaxpr/ppermute | solution.py:16
  296.4 27.2 %all_to_all.63 = bf16[2,128,4096]{2,1,0:T(8,128)(2,1)S(1)} all-to-all(bf16[2,128,4096]{2,1,0:T(8,128)(2,1)S(1)} %pad_maximum_fusion.3), channel_id=1, replica_groups=mesh['section'=4,'gx'=2,'gy'=2,'gz'=2] {'gy'}, dimensions={0} | all-to-all | bytes 4194304 | tf_op jit(solution)/shard_map/while/body/eval_jaxpr/all_to_all | solution.py:78
  340.8 34.2 %reduce-scatter.7.cloned.1.call-done = bf16[128,4096]{1,0:T(8,128)(2,1)} async-done(((bf16[256,4096]{1,0:T(8,128)(2,1)}), bf16[128,4096]{1,0:T(8,128)(2,1)}) %reduce-scatter.7.cloned.1.call-update) | async-done | bytes 1048592 | tf_op jit(solution)/shard_map/while/body/eval_jaxpr/reduce_scatter | solution.py:84
  375.5 25.0 %all-reduce.2.cloned.1.call-done = bf16[128,1024]{1,0:T(8,128)(2,1)} async-done(((bf16[128,1024]{1,0:T(8,128)(2,1)}), bf16[128,1024]{1,0:T(8,128)(2,1)}) %all-reduce.2.cloned.1.call-update) | async-done | bytes 262160 | tf_op jit(solution)/shard_map/while/body/eval_jaxpr/psum | solution.py:97
  428.1 21.4 %all-gather.6.cloned.1.call-done = bf16[256,2048]{0,1:T(8,128)(2,1)} async-done(((bf16[128,2048]{0,1:T(8,128)(2,1)}), bf16[256,2048]{0,1:T(8,128)(2,1)}) %all-gather.6.cloned.1.call-update) | async-done | bytes 1048592 | tf_op jit(solution)/shard_map/while/body/eval_jaxpr/all_gather | solution.py:141
  449.5 34.4 %all-gather.8.cloned.1.call-done = bf16[256,4096]{0,1:T(8,128)(2,1)} async-done(((bf16[256,2048]{0,1:T(8,128)(2,1)}), bf16[256,4096]{0,1:T(8,128)(2,1)}) %all-gather.8.cloned.1.call-update) | async-done | bytes 2097168 | tf_op jit(solution)/shard_map/while/body/eval_jaxpr/all_gather | solution.py:142
  494.8 16.2 %all_to_all.64 = bf16[2,128,2048]{2,1,0:T(8,128)(2,1)S(1)} all-to-all(bf16[2,128,2048]{2,1,0:T(8,128)(2,1)S(1)} %bitcast.139), channel_id=1, replica_groups=mesh['section'=4,'gx'=2,'gy'=2,'gz'=2] {'gy'}, dimensions={0} | all-to-all | bytes 2097152 | tf_op jit(solution)/shard_map/while/body/eval_jaxpr/all_to_all | solution.py:143
  524.8 11.6 %collective-permute-done = bf16[128,2048]{1,0:T(8,128)(2,1)S(1)} collective-permute-done((bf16[128,2048]{1,0:T(8,128)(2,1)S(1)}, bf16[128,2048]{1,0:T(8,128)(2,1)S(1)}, u32[]{:S(2)}, u32[]{:S(2)}) %collective-permute-start) | collective-permute-done | bytes 524320 | tf_op jit(solution)/shard_map/while/body/eval_jaxpr/ppermute | solution.py:16
  557.6 27.2 %all_to_all.63 = bf16[2,128,4096]{2,1,0:T(8,128)(2,1)S(1)} all-to-all(bf16[2,128,4096]{2,1,0:T(8,128)(2,1)S(1)} %pad_maximum_fusion.3), channel_id=1, replica_groups=mesh['section'=4,'gx'=2,'gy'=2,'gz'=2] {'gy'}, dimensions={0} | all-to-all | bytes 4194304 | tf_op jit(solution)/shard_map/while/body/eval_jaxpr/all_to_all | solution.py:78
  602.0 34.2 %reduce-scatter.7.cloned.1.call-done = bf16[128,4096]{1,0:T(8,128)(2,1)} async-done(((bf16[256,4096]{1,0:T(8,128)(2,1)}), bf16[128,4096]{1,0:T(8,128)(2,1)}) %reduce-scatter.7.cloned.1.call-update) | async-done | bytes 1048592 | tf_op jit(solution)/shard_map/while/body/eval_jaxpr/reduce_scatter | solution.py:84
  636.7 25.0 %all-reduce.2.cloned.1.call-done = bf16[128,1024]{1,0:T(8,128)(2,1)} async-done(((bf16[128,1024]{1,0:T(8,128)(2,1)}), bf16[128,1024]{1,0:T(8,128)(2,1)}) %all-reduce.2.cloned.1.call-update) | async-done | bytes 262160 | tf_op jit(solution)/shard_map/while/body/eval_jaxpr/psum | solution.py:97
  689.2 21.4 %all-gather.6.cloned.1.call-done = bf16[256,2048]{0,1:T(8,128)(2,1)} async-done(((bf16[128,2048]{0,1:T(8,128)(2,1)}), bf16[256,2048]{0,1:T(8,128)(2,1)}) %all-gather.6.cloned.1.call-update) | async-done | bytes 1048592 | tf_op jit(solution)/shard_map/while/body/eval_jaxpr/all_gather | solution.py:141
  710.7 34.6 %all-gather.8.cloned.1.call-done = bf16[256,4096]{0,1:T(8,128)(2,1)} async-done(((bf16[256,2048]{0,1:T(8,128)(2,1)}), bf16[256,4096]{0,1:T(8,128)(2,1)}) %all-gather.8.cloned.1.call-update) | async-done | bytes 2097168 | tf_op jit(solution)/shard_map/while/body/eval_jaxpr/all_gather | solution.py:142
  756.2 16.2 %all_to_all.64 = bf16[2,128,2048]{2,1,0:T(8,128)(2,1)S(1)} all-to-all(bf16[2,128,2048]{2,1,0:T(8,128)(2,1)S(1)} %bitcast.139), channel_id=1, replica_groups=mesh['section'=4,'gx'=2,'gy'=2,'gz'=2] {'gy'}, dimensions={0} | all-to-all | bytes 2097152 | tf_op jit(solution)/shard_map/while/body/eval_jaxpr/all_to_all | solution.py:143
  786.1 11.6 %collective-permute-done = bf16[128,2048]{1,0:T(8,128)(2,1)S(1)} collective-permute-done((bf16[128,2048]{1,0:T(8,128)(2,1)S(1)}, bf16[128,2048]{1,0:T(8,128)(2,1)S(1)}, u32[]{:S(2)}, u32[]{:S(2)}) %collective-permute-start) | collective-permute-done | bytes 524320 | tf_op jit(solution)/shard_map/while/body/eval_jaxpr/ppermute | solution.py:16
  819.2 27.2 %all_to_all.63 = bf16[2,128,4096]{2,1,0:T(8,128)(2,1)S(1)} all-to-all(bf16[2,128,4096]{2,1,0:T(8,128)(2,1)S(1)} %pad_maximum_fusion.3), channel_id=1, replica_groups=mesh['section'=4,'gx'=2,'gy'=2,'gz'=2] {'gy'}, dimensions={0} | all-to-all | bytes 4194304 | tf_op jit(solution)/shard_map/while/body/eval_jaxpr/all_to_all | solution.py:78
  848.6 11.5 %convolution_convert_fusion.7 = bf16[256,4096]{1,0:T(8,128)(2,1)} fusion(bf16[2048,4096]{1,0:T(8,128)(2,1)} %get-tuple-element.638, bf16[256,4096]{1,0:T(8,128)(2,1)S(1)} %bitcast.145, s32[]{:T(128)} %get-tuple-element.634), kind=kOutput, calls=%fused_computation.2.clone.1 | convolution fusion | flops 4296015872 | bytes 19922948 | tf_op jit(solution)/shard_map/while/body/eval_jaxpr/dot_general | solution.py:81
  863.7 34.0 %reduce-scatter.7.cloned.1.call-done = bf16[128,4096]{1,0:T(8,128)(2,1)} async-done(((bf16[256,4096]{1,0:T(8,128)(2,1)}), bf16[128,4096]{1,0:T(8,128)(2,1)}) %reduce-scatter.7.cloned.1.call-update) | async-done | bytes 1048592 | tf_op jit(solution)/shard_map/while/body/eval_jaxpr/reduce_scatter | solution.py:84
  898.2 25.1 %all-reduce.2.cloned.1.call-done = bf16[128,1024]{1,0:T(8,128)(2,1)} async-done(((bf16[128,1024]{1,0:T(8,128)(2,1)}), bf16[128,1024]{1,0:T(8,128)(2,1)}) %all-reduce.2.cloned.1.call-update) | async-done | bytes 262160 | tf_op jit(solution)/shard_map/while/body/eval_jaxpr/psum | solution.py:97
  950.9 21.4 %all-gather.6.cloned.1.call-done = bf16[256,2048]{0,1:T(8,128)(2,1)} async-done(((bf16[128,2048]{0,1:T(8,128)(2,1)}), bf16[256,2048]{0,1:T(8,128)(2,1)}) %all-gather.6.cloned.1.call-update) | async-done | bytes 1048592 | tf_op jit(solution)/shard_map/while/body/eval_jaxpr/all_gather | solution.py:141
  972.3 34.6 %all-gather.8.cloned.1.call-done = bf16[256,4096]{0,1:T(8,128)(2,1)} async-done(((bf16[256,2048]{0,1:T(8,128)(2,1)}), bf16[256,4096]{0,1:T(8,128)(2,1)}) %all-gather.8.cloned.1.call-update) | async-done | bytes 2097168 | tf_op jit(solution)/shard_map/while/body/eval_jaxpr/all_gather | solution.py:142
  1017.8 16.2 %all_to_all.64 = bf16[2,128,2048]{2,1,0:T(8,128)(2,1)S(1)} all-to-all(bf16[2,128,2048]{2,1,0:T(8,128)(2,1)S(1)} %bitcast.139), channel_id=1, replica_groups=mesh['section'=4,'gx'=2,'gy'=2,'gz'=2] {'gy'}, dimensions={0} | all-to-all | bytes 2097152 | tf_op jit(solution)/shard_map/while/body/eval_jaxpr/all_to_all | solution.py:143
  1047.8 11.6 %collective-permute-done = bf16[128,2048]{1,0:T(8,128)(2,1)S(1)} collective-permute-done((bf16[128,2048]{1,0:T(8,128)(2,1)S(1)}, bf16[128,2048]{1,0:T(8,128)(2,1)S(1)}, u32[]{:S(2)}, u32[]{:S(2)}) %collective-permute-start) | collective-permute-done | bytes 524320 | tf_op jit(solution)/shard_map/while/body/eval_jaxpr/ppermute | solution.py:16
  (256 shorter events, 337.0 us)
Async XLA Ops:
  14.5 64.8 %reduce-scatter.5.cloned.1.call-start = ((), (), s32[]{:S(2)}) async-start(), calls=%async_computation.7 | async-start | bytes 786432 | tf_op jit(solution)/shard_map/while/body/eval_jaxpr/reduce_scatter | solution.py:87
  64.2 49.3 %reduce-scatter.7.cloned.1.call-start = ((), (), s32[]{:S(2)}) async-start(), calls=%async_computation.9 | async-start | bytes 3145728 | tf_op jit(solution)/shard_map/while/body/eval_jaxpr/reduce_scatter | solution.py:84
  75.8 63.2 %all-reduce.2.cloned.1.call-start = ((), (), s32[]{:S(2)}) async-start(), calls=%async_computation.8 | async-start | bytes 524288 | tf_op jit(solution)/shard_map/while/body/eval_jaxpr/psum | solution.py:97
  79.3 82.2 %reduce-scatter.9.cloned.1.call-start = ((), (), s32[]{:S(2)}) async-start(), calls=%async_computation.10 | async-start | bytes 1572864 | tf_op jit(solution)/shard_map/while/body/eval_jaxpr/reduce_scatter | solution.py:92
  113.5 74.2 %all-gather.6.cloned.1.call-start = ((), (), s32[]{:S(2)}) async-start(), calls=%async_computation.11 | async-start | bytes 1572864 | tf_op jit(solution)/shard_map/while/body/eval_jaxpr/all_gather | solution.py:141
  166.4 56.1 %all-gather.8.cloned.1.call-start = ((), (), s32[]{:S(2)}) async-start(), calls=%async_computation.12 | async-start | bytes 3145728 | tf_op jit(solution)/shard_map/while/body/eval_jaxpr/all_gather | solution.py:142
  187.8 70.4 %reduce-scatter.11.cloned.1.call-start = ((), (), s32[]{:S(2)}) async-start(), calls=%async_computation.13 | async-start | bytes 1572864 | tf_op jit(solution)/shard_map/while/body/eval_jaxpr/reduce_scatter | solution.py:166
  259.6 15.3 %collective-permute-start = (bf16[128,2048]{1,0:T(8,128)(2,1)S(1)}, bf16[128,2048]{1,0:T(8,128)(2,1)S(1)}, u32[]{:S(2)}, u32[]{:S(2)}) collective-permute-start(bf16[128,2048]{1,0:T(8,128)(2,1)S(1)} %get-tuple-element.592), channel_id=1, source_target_pairs={{0,8},{8,16},{16,24},{1,9},{9,17},{17,25},{2,10},{10,18},{18,26},{... | collective-permute-start | bytes 1572872 | tf_op jit(solution)/shard_map/while/body/eval_jaxpr/ppermute | solution.py:16
  276.8 64.0 %reduce-scatter.5.cloned.1.call-start = ((), (), s32[]{:S(2)}) async-start(), calls=%async_computation.7 | async-start | bytes 786432 | tf_op jit(solution)/shard_map/while/body/eval_jaxpr/reduce_scatter | solution.py:87
  325.7 49.3 %reduce-scatter.7.cloned.1.call-start = ((), (), s32[]{:S(2)}) async-start(), calls=%async_computation.9 | async-start | bytes 3145728 | tf_op jit(solution)/shard_map/while/body/eval_jaxpr/reduce_scatter | solution.py:84
  337.3 63.2 %all-reduce.2.cloned.1.call-start = ((), (), s32[]{:S(2)}) async-start(), calls=%async_computation.8 | async-start | bytes 524288 | tf_op jit(solution)/shard_map/while/body/eval_jaxpr/psum | solution.py:97
  340.8 82.3 %reduce-scatter.9.cloned.1.call-start = ((), (), s32[]{:S(2)}) async-start(), calls=%async_computation.10 | async-start | bytes 1572864 | tf_op jit(solution)/shard_map/while/body/eval_jaxpr/reduce_scatter | solution.py:92
  375.0 74.4 %all-gather.6.cloned.1.call-start = ((), (), s32[]{:S(2)}) async-start(), calls=%async_computation.11 | async-start | bytes 1572864 | tf_op jit(solution)/shard_map/while/body/eval_jaxpr/all_gather | solution.py:141
  428.0 55.9 %all-gather.8.cloned.1.call-start = ((), (), s32[]{:S(2)}) async-start(), calls=%async_computation.12 | async-start | bytes 3145728 | tf_op jit(solution)/shard_map/while/body/eval_jaxpr/all_gather | solution.py:142
  449.4 70.3 %reduce-scatter.11.cloned.1.call-start = ((), (), s32[]{:S(2)}) async-start(), calls=%async_computation.13 | async-start | bytes 1572864 | tf_op jit(solution)/shard_map/while/body/eval_jaxpr/reduce_scatter | solution.py:166
  521.1 15.3 %collective-permute-start = (bf16[128,2048]{1,0:T(8,128)(2,1)S(1)}, bf16[128,2048]{1,0:T(8,128)(2,1)S(1)}, u32[]{:S(2)}, u32[]{:S(2)}) collective-permute-start(bf16[128,2048]{1,0:T(8,128)(2,1)S(1)} %get-tuple-element.592), channel_id=1, source_target_pairs={{0,8},{8,16},{16,24},{1,9},{9,17},{17,25},{2,10},{10,18},{18,26},{... | collective-permute-start | bytes 1572872 | tf_op jit(solution)/shard_map/while/body/eval_jaxpr/ppermute | solution.py:16
  538.3 63.7 %reduce-scatter.5.cloned.1.call-start = ((), (), s32[]{:S(2)}) async-start(), calls=%async_computation.7 | async-start | bytes 786432 | tf_op jit(solution)/shard_map/while/body/eval_jaxpr/reduce_scatter | solution.py:87
  586.9 49.3 %reduce-scatter.7.cloned.1.call-start = ((), (), s32[]{:S(2)}) async-start(), calls=%async_computation.9 | async-start | bytes 3145728 | tf_op jit(solution)/shard_map/while/body/eval_jaxpr/reduce_scatter | solution.py:84
  598.5 63.1 %all-reduce.2.cloned.1.call-start = ((), (), s32[]{:S(2)}) async-start(), calls=%async_computation.8 | async-start | bytes 524288 | tf_op jit(solution)/shard_map/while/body/eval_jaxpr/psum | solution.py:97
  602.0 82.3 %reduce-scatter.9.cloned.1.call-start = ((), (), s32[]{:S(2)}) async-start(), calls=%async_computation.10 | async-start | bytes 1572864 | tf_op jit(solution)/shard_map/while/body/eval_jaxpr/reduce_scatter | solution.py:92
  636.2 74.4 %all-gather.6.cloned.1.call-start = ((), (), s32[]{:S(2)}) async-start(), calls=%async_computation.11 | async-start | bytes 1572864 | tf_op jit(solution)/shard_map/while/body/eval_jaxpr/all_gather | solution.py:141
  689.2 56.1 %all-gather.8.cloned.1.call-start = ((), (), s32[]{:S(2)}) async-start(), calls=%async_computation.12 | async-start | bytes 3145728 | tf_op jit(solution)/shard_map/while/body/eval_jaxpr/all_gather | solution.py:142
  710.6 70.4 %reduce-scatter.11.cloned.1.call-start = ((), (), s32[]{:S(2)}) async-start(), calls=%async_computation.13 | async-start | bytes 1572864 | tf_op jit(solution)/shard_map/while/body/eval_jaxpr/reduce_scatter | solution.py:166
  782.4 15.3 %collective-permute-start = (bf16[128,2048]{1,0:T(8,128)(2,1)S(1)}, bf16[128,2048]{1,0:T(8,128)(2,1)S(1)}, u32[]{:S(2)}, u32[]{:S(2)}) collective-permute-start(bf16[128,2048]{1,0:T(8,128)(2,1)S(1)} %get-tuple-element.592), channel_id=1, source_target_pairs={{0,8},{8,16},{16,24},{1,9},{9,17},{17,25},{2,10},{10,18},{18,26},{... | collective-permute-start | bytes 1572872 | tf_op jit(solution)/shard_map/while/body/eval_jaxpr/ppermute | solution.py:16
  799.6 64.0 %reduce-scatter.5.cloned.1.call-start = ((), (), s32[]{:S(2)}) async-start(), calls=%async_computation.7 | async-start | bytes 786432 | tf_op jit(solution)/shard_map/while/body/eval_jaxpr/reduce_scatter | solution.py:87
  848.6 49.1 %reduce-scatter.7.cloned.1.call-start = ((), (), s32[]{:S(2)}) async-start(), calls=%async_computation.9 | async-start | bytes 3145728 | tf_op jit(solution)/shard_map/while/body/eval_jaxpr/reduce_scatter | solution.py:84
  860.2 63.1 %all-reduce.2.cloned.1.call-start = ((), (), s32[]{:S(2)}) async-start(), calls=%async_computation.8 | async-start | bytes 524288 | tf_op jit(solution)/shard_map/while/body/eval_jaxpr/psum | solution.py:97
  863.7 82.3 %reduce-scatter.9.cloned.1.call-start = ((), (), s32[]{:S(2)}) async-start(), calls=%async_computation.10 | async-start | bytes 1572864 | tf_op jit(solution)/shard_map/while/body/eval_jaxpr/reduce_scatter | solution.py:92
  897.7 74.6 %all-gather.6.cloned.1.call-start = ((), (), s32[]{:S(2)}) async-start(), calls=%async_computation.11 | async-start | bytes 1572864 | tf_op jit(solution)/shard_map/while/body/eval_jaxpr/all_gather | solution.py:141
  950.9 56.1 %all-gather.8.cloned.1.call-start = ((), (), s32[]{:S(2)}) async-start(), calls=%async_computation.12 | async-start | bytes 3145728 | tf_op jit(solution)/shard_map/while/body/eval_jaxpr/all_gather | solution.py:142
  972.3 70.4 %reduce-scatter.11.cloned.1.call-start = ((), (), s32[]{:S(2)}) async-start(), calls=%async_computation.13 | async-start | bytes 1572864 | tf_op jit(solution)/shard_map/while/body/eval_jaxpr/reduce_scatter | solution.py:166
  1044.1 15.3 %collective-permute-start = (bf16[128,2048]{1,0:T(8,128)(2,1)S(1)}, bf16[128,2048]{1,0:T(8,128)(2,1)S(1)}, u32[]{:S(2)}, u32[]{:S(2)}) collective-permute-start(bf16[128,2048]{1,0:T(8,128)(2,1)S(1)} %get-tuple-element.592), channel_id=1, source_target_pairs={{0,8},{8,16},{16,24},{1,9},{9,17},{17,25},{2,10},{10,18},{18,26},{... | collective-permute-start | bytes 1572872 | tf_op jit(solution)/shard_map/while/body/eval_jaxpr/ppermute | solution.py:16
  (17 other events, 205.3 us)
Sparse Core Ops, SparseCore 0:
  14.9 11.7 all-gather.3
  64.3 14.8 reduce-scatter.4
  81.5 31.9 reduce-scatter.6
  115.6 23.2 all-reduce.1
  141.1 20.3 reduce-scatter.8
  166.5 21.2 all-gather.5
  189.3 33.0 all-gather.7
  250.7 7.4 reduce-scatter.10
  277.2 10.9 all-gather.3
  325.8 14.8 reduce-scatter.4
  343.0 31.9 reduce-scatter.6
  377.1 23.2 all-reduce.1
  402.7 20.3 reduce-scatter.8
  428.1 21.2 all-gather.5
  450.8 33.0 all-gather.7
  512.2 7.4 reduce-scatter.10
  538.4 10.9 all-gather.3
  587.0 14.8 reduce-scatter.4
  604.2 31.9 reduce-scatter.6
  638.3 23.2 all-reduce.1
  663.9 20.3 reduce-scatter.8
  689.3 21.2 all-gather.5
  712.2 33.0 all-gather.7
  773.5 7.4 reduce-scatter.10
  800.1 10.9 all-gather.3
  848.7 14.8 reduce-scatter.4
  865.7 31.9 reduce-scatter.6
  900.0 23.2 all-reduce.1
  925.5 20.3 reduce-scatter.8
  951.0 21.2 all-gather.5
  973.8 33.0 all-gather.7
  1035.2 7.4 reduce-scatter.10
